TPU v7x, 32 devices: a whole 2x2x4 slice. The times are simulated.
32 devices in a mesh: dp: 8 (over y, x, core), tensor: 4 (over z).
Axes of the slice: x: 2, y: 2, z: 4, core: 2. Of those that a mesh axis runs over, the one named last changes fastest.
Arguments:
- node_features: bfloat16 [8192, 768], P(('dp', 'tensor')), may hold values from -6 to 6
- graph_ids: int32 [64, 128], P('dp'), may hold values from 0 to 5, never falling along the last dimension, each value on 1 to 32 neighbouring positions
- degree: int32 [8192], P(('dp', 'tensor')), may hold values from 0 to 511
- distance: int32 [8192, 128], P('dp'), may hold values from 0 to 511
- out_grad: bfloat16 [8192, 768], P(('dp', 'tensor')), may hold values from -6 to 6
- qkv_weight: bfloat16 [3, 768, 768], P(None, 'tensor'), may hold values from -0.21875 to 0.21875
- qv_bias: float32 [2, 768], P(None, 'tensor'), may hold values from -3 to 3
- out_weight: bfloat16 [768, 768], P('tensor'), may hold values from -0.625 to 0.625
- out_bias: float32 [768], replicated, may hold values from -3 to 3
- norm1_gain: float32 [768], replicated, may hold values from 0.5 to 1.5
- norm1_shift: float32 [768], replicated, may hold values from -2 to 2
- ffn_in_weight: bfloat16 [768, 768], P('tensor'), may hold values from -0.21875 to 0.21875
- ffn_in_bias: float32 [768], P('tensor'), may hold values from -3 to 3
- ffn_out_weight: bfloat16 [768, 768], P('tensor'), may hold values from -0.21875 to 0.21875
- ffn_out_bias: float32 [768], replicated, may hold values from -3 to 3
- norm2_gain: float32 [768], replicated, may hold values from 0.5 to 1.5
- norm2_shift: float32 [768], replicated, may hold values from -2 to 2
- degree_table: bfloat16 [512, 768], replicated, may hold values from -3 to 3
- spatial_table: bfloat16 [32, 512], P('tensor'), may hold values from -4 to 4
Outputs:
- layer_out: bfloat16 [8192, 768], P(('dp', 'tensor'))
- input_grad: bfloat16 [8192, 768], P(('dp', 'tensor'))
- qkv_weight_grad: float32 [3, 768, 768], P(None, 'tensor')
- qv_bias_grad: float32 [2, 768], P(None, 'tensor')
- out_weight_grad: float32 [768, 768], P('tensor')
- out_bias_grad: float32 [768], replicated
- norm1_gain_grad: float32 [768], replicated
- norm1_shift_grad: float32 [768], replicated
- ffn_in_weight_grad: float32 [768, 768], P('tensor')
- ffn_in_bias_grad: float32 [768], P('tensor')
- ffn_out_weight_grad: float32 [768, 768], P('tensor')
- ffn_out_bias_grad: float32 [768], replicated
- norm2_gain_grad: float32 [768], replicated
- norm2_shift_grad: float32 [768], replicated
- degree_table_grad: float32 [512, 768], replicated
- spatial_table_grad: float32 [32, 512], P('tensor')
Inputs may be any that keep to these rules, and one draw needn't show every extreme that they name: `graph_ids`: graph numbers never fall along a packed block; a graph holds at most a quarter of 128 nodes, and in every block some graph holds exactly that many.
All inputs are finite; a program needn't handle non-finite values.
Results may differ from a plain program's by a relative error of at most 0.018.
Values may be sent and summed in bfloat16 or wider, within the bound.
A program may use at most 128 MiB of HBM per device.

v0:
```python
import functools
import math

import jax
import jax.numpy as jnp
from jax import lax
from jax.experimental import pallas as pl
from jax.experimental.pallas import tpu as pltpu
from jax.sharding import PartitionSpec as P

norm_eps = 1e-05
masked_score = -1e30
MESH = pl.DeviceIdType.MESH
WEIGHTS = 6


def against_cols(left, right):
    return lax.dot_general(
        left, right, (((1,), (1,)), ((), ())), preferred_element_type=jnp.float32
    )


def place():
    dp = lax.axis_index("dp")
    tensor = lax.axis_index("tensor")
    core = lax.rem(dp, 2)
    bit_x = lax.rem(dp // 2, 2)
    bit_y = lax.rem(dp // 4, 2)
    return dp, tensor, core, bit_x, bit_y


def partners(dp, core, bit_x, bit_y):
    return dp + 1 - 2 * core, dp + 2 - 4 * bit_x, dp + 4 - 8 * bit_y


def greet(devices):
    barrier = pltpu.get_barrier_semaphore()
    for device in devices:
        pl.semaphore_signal(barrier, inc=1, device_id=device, device_id_type=MESH)
    pl.semaphore_wait(barrier, len(devices))


def send(source, target, send_sem, recv_sem, device):
    copy = pltpu.make_async_remote_copy(
        src_ref=source,
        dst_ref=target,
        send_sem=send_sem,
        recv_sem=recv_sem,
        device_id=device,
        device_id_type=MESH,
    )
    copy.start()
    return copy


def gather_kernel(
    planes,
    half,
    qkv,
    out_w,
    in_w,
    ffn_w,
    table,
    bias,
    full,
    tables,
    biases,
    send_sem,
    recv_sem,
    small_send,
    small_recv,
    own_sem,
):
    dp, tensor, core, bit_x, bit_y = place()
    across_core, across_x, across_y = partners(dp, core, bit_x, bit_y)
    greet(
        [(across_core, tensor), (across_x, tensor), (across_y, tensor)]
        + [(dp, lax.rem(tensor + k, planes)) for k in range(1, planes)]
    )
    lanes = pl.ds(pl.multiple_of(core * half, half), half)
    shards = [qkv.at[0], qkv.at[1], qkv.at[2], out_w, in_w, ffn_w]
    started = []
    small = []
    for k in range(1, planes):
        other = lax.rem(tensor + k, planes)
        for n, (own, whole) in enumerate(((table, tables), (bias, biases))):
            small.append(
                send(
                    own,
                    whole.at[tensor],
                    small_send.at[n, k - 1],
                    small_recv.at[n, k - 1],
                    (dp, other),
                )
            )
    locals_ = [
        pltpu.make_async_copy(table, tables.at[tensor], own_sem.at[WEIGHTS]),
        pltpu.make_async_copy(bias, biases.at[tensor], own_sem.at[WEIGHTS + 1]),
    ]
    stage_z, stage_a, stage_b, stage_c = {}, {}, {}, {}
    for w in range(WEIGHTS):
        first, second = (bit_x, bit_y) if w % 2 == 0 else (bit_y, bit_x)
        for k in range(1, planes):
            other = lax.rem(tensor + k, planes)
            stage_z[w, k] = send(
                shards[w].at[first, second, :, lanes],
                full.at[w, tensor, first, second, :, lanes],
                send_sem.at[0, w, k - 1],
                recv_sem.at[0, w, k - 1],
                (dp, other),
            )
    for w in range(WEIGHTS):
        locals_.append(pltpu.make_async_copy(shards[w], full.at[w, tensor], own_sem.at[w]))
    for copy in locals_:
        copy.start()
    for w in range(WEIGHTS):
        first, second = (bit_x, bit_y) if w % 2 == 0 else (bit_y, bit_x)
        across = across_y if w % 2 == 0 else across_x
        for k in range(1, planes):
            stage_z[w, k].wait_recv()
            whose = lax.rem(tensor + planes - k, planes)
            region = full.at[w, whose, first, second, :, lanes]
            stage_a[w, k] = send(
                region, region, send_sem.at[1, w, k - 1], recv_sem.at[1, w, k - 1], (across, tensor)
            )
    for w in range(WEIGHTS):
        first = bit_x if w % 2 == 0 else bit_y
        across = across_x if w % 2 == 0 else across_y
        for k in range(1, planes):
            stage_a[w, k].wait_recv()
            whose = lax.rem(tensor + planes - k, planes)
            region = full.at[w, whose, first, :, :, lanes]
            stage_b[w, k] = send(
                region, region, send_sem.at[2, w, k - 1], recv_sem.at[2, w, k - 1], (across, tensor)
            )
    for w in range(WEIGHTS):
        for k in range(1, planes):
            stage_b[w, k].wait_recv()
            whose = lax.rem(tensor + planes - k, planes)
            region = full.at[w, whose, :, :, :, lanes]
            stage_c[w, k] = send(
                region,
                region,
                send_sem.at[3, w, k - 1],
                recv_sem.at[3, w, k - 1],
                (across_core, tensor),
            )
    for copy in small:
        copy.wait_recv()
    for copy in stage_c.values():
        copy.wait_recv()
    for copy in locals_:
        copy.wait()
    for stage in (stage_z, stage_a, stage_b, stage_c):
        for copy in stage.values():
            copy.wait_send()
    for copy in small:
        copy.wait_send()


def gather_weights(planes, qkv, out_w, in_w, ffn_w, table, bias):
    shard_rows, width = out_w.shape
    part = shard_rows // 4
    half = width // 2

    def split(matrix):
        return matrix.reshape(matrix.shape[:-2] + (2, 2, part, width))

    vmem = pl.BlockSpec(memory_space=pltpu.VMEM)
    full, tables, biases = pl.pallas_call(
        functools.partial(gather_kernel, planes, half),
        out_shape=(
            jax.ShapeDtypeStruct((WEIGHTS, planes, 2, 2, part, width), jnp.bfloat16),
            jax.ShapeDtypeStruct((planes,) + table.shape, jnp.bfloat16),
            jax.ShapeDtypeStruct((planes,) + bias.shape, jnp.float32),
        ),
        in_specs=[vmem] * 6,
        out_specs=(vmem,) * 3,
        scratch_shapes=[
            pltpu.SemaphoreType.DMA((4, WEIGHTS, planes - 1)),
            pltpu.SemaphoreType.DMA((4, WEIGHTS, planes - 1)),
            pltpu.SemaphoreType.DMA((2, planes - 1)),
            pltpu.SemaphoreType.DMA((2, planes - 1)),
            pltpu.SemaphoreType.DMA((WEIGHTS + 2,)),
        ],
        compiler_params=pltpu.CompilerParams(collective_id=0, has_side_effects=True),
        name="gather_weights",
    )(split(qkv), split(out_w), split(in_w), split(ffn_w), table, bias)
    return (
        full.reshape(WEIGHTS, planes * shard_rows, width),
        tables.reshape(-1, table.shape[1]),
        biases.transpose(1, 0, 2).reshape(bias.shape[0], -1),
    )


def add_into(target, left, right):
    target[...] = (left[...].astype(jnp.float32) + right[...].astype(jnp.float32)).astype(target.dtype)


def reduce_kernel(
    planes,
    groups,
    grads,
    table,
    small,
    fin,
    fin_table,
    fin_small,
    recv_c,
    recv_a,
    recv_b,
    recv_z,
    recv_g,
    sum_c,
    sum_a,
    sum_b,
    trecv_c,
    trecv_a,
    trecv_b,
    trecv_z,
    trecv_g,
    tsum_c,
    tsum_a,
    tsum_b,
    srecv_c,
    srecv_a,
    srecv_b,
    srecv_z,
    srecv_g,
    ssum_a,
    ssum_b,
    ssum_z,
    ssum_g,
    send_sem,
    recv_sem,
):
    dp, tensor, core, bit_x, bit_y = place()
    across_core, across_x, across_y = partners(dp, core, bit_x, bit_y)
    group = dp // 8
    rest = [lax.rem(group + k, groups) * 8 + lax.rem(dp, 8) for k in range(1, groups)]
    greet(
        [(across_core, tensor), (across_x, tensor), (across_y, tensor)]
        + [(dp, lax.rem(tensor + k, planes)) for k in range(1, planes)]
        + [(other, tensor) for other in rest]
    )
    jobs = []
    copies = []
    counter = [0]

    def push(source, target, device):
        n = counter[0]
        counter[0] += 1
        copy = send(source, target, send_sem.at[n], recv_sem.at[n], device)
        copies.append(copy)
        return copy

    def small_job():
        copy = push(small, srecv_c, (across_core, tensor))
        yield
        copy.wait_recv()
        add_into(ssum_a, small, srecv_c)
        copy = push(ssum_a, srecv_a, (across_x, tensor))
        yield
        copy.wait_recv()
        add_into(ssum_b, ssum_a, srecv_a)
        copy = push(ssum_b, srecv_b, (across_y, tensor))
        yield
        copy.wait_recv()
        add_into(ssum_z, ssum_b, srecv_b)
        srecv_z[tensor] = ssum_z[...]
        sent = [
            push(ssum_z, srecv_z.at[tensor], (dp, lax.rem(tensor + k, planes)))
            for k in range(1, planes)
        ]
        yield
        for copy in sent:
            copy.wait_recv()
        total = srecv_z[0].astype(jnp.float32)
        for k in range(1, planes):
            total = total + srecv_z[k].astype(jnp.float32)
        if groups > 1:
            ssum_g[...] = total.astype(jnp.bfloat16)
            srecv_g[group] = ssum_g[...]
            sent = [push(ssum_g, srecv_g.at[group], (other, tensor)) for other in rest]
            for copy in sent:
                copy.wait_recv()
            total = srecv_g[0].astype(jnp.float32)
            for k in range(1, groups):
                total = total + srecv_g[k].astype(jnp.float32)
        fin_small[...] = total

    def matrix_job(w, whole, parts, bufs, spread):
        c_in, a_in, b_in, z_in, g_in, c_sum, a_sum, b_sum = bufs
        x_first = w % 2 == 0
        first, second = (bit_x, bit_y) if x_first else (bit_y, bit_x)
        to_first, to_second = (across_x, across_y) if x_first else (across_y, across_x)
        copy = push(whole.at[1 - core], c_in, (across_core, tensor))
        yield
        copy.wait_recv()
        own = whole.at[core]
        for p in range(planes):
            add_into(c_sum.at[:, :, p], own.at[:, :, p], c_in.at[:, :, p])
        copy = push(c_sum.at[1 - first], a_in, (to_first, tensor))
        yield
        copy.wait_recv()
        for q in range(2):
            add_into(a_sum.at[q], c_sum.at[first, q], a_in.at[q])
        copy = push(a_sum.at[1 - second], b_in, (to_second, tensor))
        yield
        copy.wait_recv()
        add_into(b_sum, a_sum.at[second], b_in)
        sent = []
        for k in range(1, planes):
            other = lax.rem(tensor + k, planes)
            sent.append(push(b_sum.at[other], z_in.at[k - 1], (dp, other)))
        yield
        for copy in sent:
            copy.wait_recv()
        total = b_sum[tensor].astype(jnp.float32)
        for k in range(1, planes):
            total = total + z_in[k - 1].astype(jnp.float32)
        mine = parts.at[core, first, second, tensor] if spread else parts.at[core, first, second]
        mine[...] = total.astype(jnp.bfloat16)
        if groups > 1:
            g_in[group] = mine[...]
            sent = [push(mine, g_in.at[group], (other, tensor)) for other in rest]
            for copy in sent:
                copy.wait_recv()
            total = g_in[0].astype(jnp.float32)
            for k in range(1, groups):
                total = total + g_in[k].astype(jnp.float32)
            for copy in sent:
                copy.wait_send()
            mine[...] = total.astype(jnp.bfloat16)
        if spread:
            sent = [
                push(mine, mine, (dp, lax.rem(tensor + k, planes))) for k in range(1, planes)
            ]
            yield
            for copy in sent:
                copy.wait_recv()
        region = parts.at[core, first, second]
        copy = push(region, region, (to_second, tensor))
        yield
        copy.wait_recv()
        region = parts.at[core, first]
        copy = push(region, region, (to_first, tensor))
        yield
        copy.wait_recv()
        region = parts.at[core]
        copy = push(region, region, (across_core, tensor))
        yield
        copy.wait_recv()

    jobs.append(small_job())
    jobs.append(
        matrix_job(
            0,
            table,
            fin_table,
            (trecv_c, trecv_a, trecv_b, trecv_z, trecv_g, tsum_c, tsum_a, tsum_b),
            True,
        )
    )
    for w in range(WEIGHTS):
        jobs.append(
            matrix_job(
                w,
                grads.at[w],
                fin.at[w],
                (
                    recv_c.at[w],
                    recv_a.at[w],
                    recv_b.at[w],
                    recv_z.at[w],
                    recv_g.at[w] if groups > 1 else None,
                    sum_c.at[w],
                    sum_a.at[w],
                    sum_b.at[w],
                ),
                False,
            )
        )
    while jobs:
        left = []
        for job in jobs:
            try:
                next(job)
                left.append(job)
            except StopIteration:
                pass
        jobs = left
    for copy in copies:
        copy.wait_send()


def reduce_all(planes, groups, grads, table, small):
    part, half = grads.shape[-2:]
    tpart = table.shape[-2]
    bf = jnp.bfloat16
    vmem = pl.BlockSpec(memory_space=pltpu.VMEM)
    spare = max(groups, 1)

    def many(lead, rows):
        return [
            pltpu.VMEM(lead + (2, 2, planes, rows, half), bf),
            pltpu.VMEM(lead + (2, planes, rows, half), bf),
            pltpu.VMEM(lead + (planes, rows, half), bf),
            pltpu.VMEM(lead + (planes - 1, rows, half), bf),
            pltpu.VMEM(lead + (spare, rows, half), bf),
            pltpu.VMEM(lead + (2, 2, planes, rows, half), bf),
            pltpu.VMEM(lead + (2, planes, rows, half), bf),
            pltpu.VMEM(lead + (planes, rows, half), bf),
        ]

    small_buf = pltpu.VMEM(small.shape, bf)
    rest = groups - 1
    sends = WEIGHTS * (6 + planes - 1 + rest) + (6 + 2 * (planes - 1) + rest) + 3 + planes - 1 + rest
    return pl.pallas_call(
        functools.partial(reduce_kernel, planes, groups),
        out_shape=(
            jax.ShapeDtypeStruct((WEIGHTS, 2, 2, 2, part, half), bf),
            jax.ShapeDtypeStruct((2, 2, 2, planes, tpart, half), bf),
            jax.ShapeDtypeStruct(small.shape, jnp.float32),
        ),
        in_specs=[vmem] * 3,
        out_specs=(vmem,) * 3,
        scratch_shapes=many((WEIGHTS,), part)
        + many((), tpart)
        + [
            small_buf,
            small_buf,
            small_buf,
            pltpu.VMEM((planes,) + small.shape, bf),
            pltpu.VMEM((spare,) + small.shape, bf),
            small_buf,
            small_buf,
            small_buf,
            small_buf,
            pltpu.SemaphoreType.DMA((sends,)),
            pltpu.SemaphoreType.DMA((sends,)),
        ],
        compiler_params=pltpu.CompilerParams(collective_id=1, has_side_effects=True),
        name="reduce_grads",
    )(grads, table, small)


def transposed_left(left, right):
    return lax.dot_general(
        left, right, (((0,), (0,)), ((), ())), preferred_element_type=jnp.float32
    )


def plain(left, right):
    return lax.dot_general(
        left, right, (((1,), (0,)), ((), ())), preferred_element_type=jnp.float32
    )


def normalized(rows):
    row_mean = jnp.mean(rows, axis=1, keepdims=True)
    centered = rows - row_mean
    variance = jnp.mean(centered * centered, axis=1, keepdims=True)
    inverse = lax.rsqrt(variance + norm_eps)
    return centered * inverse, inverse


def layer_kernel(
    shape,
    features,
    graph_ids,
    degree,
    distance,
    out_grad,
    weights,
    table,
    bias,
    vectors,
    degree_table,
    layer_out,
    input_grad,
    grads,
    table_grad,
    small,
    embedded,
    normed,
    act,
    qkv,
    mixed,
    soft,
    scores_grad,
    fold_low,
    fold_high,
    fold_same,
    residual,
    second,
    act2,
    mixed_grad,
    stacked,
    pre_act,
    bias_cols,
):
    planes, heads, head_dim, block, half = shape
    rows, width = features.shape
    blocks = rows // block
    fold = block // 2
    scale = 1.0 / math.sqrt(head_dim)
    bf = jnp.bfloat16
    f32 = jnp.float32
    tensor = lax.axis_index("tensor")
    out_bias, gain1, shift1, ffn_bias, gain2, shift2 = (vectors[pl.ds(n, 1), :] for n in range(6))

    onehot = (
        lax.broadcasted_iota(jnp.int32, (degree_table.shape[0], rows), 0) == degree[...]
    ).astype(f32).astype(bf)
    embedded[...] = features[...].astype(f32) + transposed_left(onehot, degree_table[...])
    first, inverse1 = normalized(embedded[...])
    normed[...] = first
    act[...] = (first * gain1 + shift1).astype(bf)

    position = lax.broadcasted_iota(jnp.int32, (fold, block), 0)
    lane = lax.broadcasted_iota(jnp.int32, (fold, block), 1)
    inside = jnp.abs(lane - position) < block // 4

    def folded(square):
        return jnp.where(inside, square[:fold], square[fold:])

    def unfolded(part):
        zero = jnp.zeros_like(part)
        return jnp.concatenate(
            [jnp.where(inside, part, zero), jnp.where(inside, zero, part)], axis=0
        ).astype(bf)

    for g in range(blocks):
        start = pl.multiple_of(tensor * rows + g * block, block)
        index = folded(jnp.transpose(distance[pl.ds(start, block), :]))
        lanes = pl.ds(g * block, block)
        fold_low[:, lanes] = lax.rem(index, 128)
        fold_high[:, lanes] = index // 128
        across = jnp.broadcast_to(graph_ids[pl.ds(tensor * blocks + g, 1), :], (block, block))
        down = folded(jnp.transpose(across))
        fold_same[:, lanes] = jnp.where(down == across[:fold], 1, 0)

    bias_cols[...] = jnp.transpose(bias[...])
    act_rows = act[...]
    for k in range(3):
        part = against_cols(weights[k], act_rows)
        if k != 1:
            column = 0 if k == 0 else 1
            part = part + bias_cols[:, column : column + 1]
        qkv[k] = part

    def head_rows(h):
        return pl.ds(pl.multiple_of(h * head_dim, 8), head_dim)

    def forward(h, carry):
        for g in range(blocks):
            lanes = pl.ds(g * block, block)
            q = qkv[0, head_rows(h), lanes].astype(bf)
            k = qkv[1, head_rows(h), lanes].astype(bf)
            v = qkv[2, head_rows(h), lanes].astype(bf)
            raw = folded(transposed_left(k, q))
            low = fold_low[:, lanes]
            high = fold_high[:, lanes]
            looked = None
            for c in range(table.shape[1]):
                source = jnp.broadcast_to(table[h, pl.ds(c, 1), :], (fold, 128))
                found = jnp.take_along_axis(source, low, axis=1, mode="promise_in_bounds")
                looked = found if c == 0 else jnp.where(high == c, found, looked)
            scores = jnp.where(fold_same[:, lanes] == 1, raw * scale + looked, masked_score)
            shifted = jnp.exp(scores - jnp.max(scores, axis=0, keepdims=True))
            part = shifted * (1.0 / jnp.sum(shifted, axis=0, keepdims=True))
            soft[g * heads + h] = part
            mixed[head_rows(h), lanes] = plain(v, unfolded(part))
        return carry

    lax.fori_loop(0, heads, forward, 0, unroll=2)

    mixed_low = mixed[...].astype(bf)
    residual[...] = embedded[...] + transposed_left(mixed_low, weights[3]) + out_bias
    again, inverse2 = normalized(residual[...])
    second[...] = again
    act2[...] = (again * gain2 + shift2).astype(bf)
    pre_act[...] = against_cols(act2[...], weights[4]) + bias[pl.ds(2, 1), :]
    upward = pre_act[...]
    bell = 0.5 * (1.0 + lax.erf(upward * (1.0 / math.sqrt(2.0))))
    hidden = (upward * bell).astype(bf)
    layer_out[...] = (residual[...] + plain(hidden, weights[5]) + ffn_bias).astype(bf)
    grad_low = out_grad[...]
    hidden_grad = against_cols(grad_low, weights[5])
    slope = bell + upward * jnp.exp(-0.5 * upward * upward) * (1.0 / math.sqrt(2.0 * math.pi))
    pre_grad = (hidden_grad * slope).astype(bf)

    part = grads.shape[-2]

    def keep(target, matrix, rows_each):
        low = matrix.astype(bf)
        for p in range(planes):
            for a in range(2):
                for b in range(2):
                    at = ((p * 2 + a) * 2 + b) * rows_each
                    for c in range(2):
                        target[c, a, b, p] = low[at : at + rows_each, c * half : (c + 1) * half]

    keep(grads.at[5], transposed_left(hidden, grad_low), part)
    keep(grads.at[4], transposed_left(pre_grad, act2[...]), part)
    small[...] = jnp.zeros_like(small)
    table_width = table.shape[1] * 128

    def note(row, values):
        small[pl.ds(heads + row, 1), :] = values

    def down_sum(values):
        return jnp.sum(values, axis=0, keepdims=True)

    note(2, down_sum(pre_grad.astype(f32)))
    upstream = grad_low.astype(f32)
    note(6, down_sum(upstream))
    normed2_grad = plain(pre_grad, weights[4])

    def norm_through(grad, unit, inverse, gain):
        scaled = grad * gain
        first_mean = jnp.mean(scaled, axis=1, keepdims=True)
        second_mean = jnp.mean(scaled * unit, axis=1, keepdims=True)
        return inverse * (scaled - first_mean - unit * second_mean)

    note(7, down_sum(normed2_grad * second[...]))
    note(8, down_sum(normed2_grad))
    residual_grad = upstream + norm_through(normed2_grad, second[...], inverse2, gain2)
    residual[...] = residual_grad
    note(3, down_sum(residual_grad))
    attn_grad = residual_grad.astype(bf)
    keep(grads.at[3], plain(mixed_low, attn_grad), part)
    mixed_grad[...] = against_cols(weights[3], attn_grad)

    def backward(h, carry):
        for g in range(blocks):
            lanes = pl.ds(g * block, block)
            q = qkv[0, head_rows(h), lanes].astype(bf)
            k = qkv[1, head_rows(h), lanes].astype(bf)
            v = qkv[2, head_rows(h), lanes].astype(bf)
            d = mixed_grad[head_rows(h), lanes].astype(bf)
            probs = soft[g * heads + h]
            weighted = probs * folded(transposed_left(v, d))
            change = weighted - probs * jnp.sum(weighted, axis=0, keepdims=True)
            change_low = change.astype(bf).astype(f32)
            scores_grad[g, pl.ds(h, fold, stride=heads), :] = change_low
            change_full = unfolded(change_low)
            stacked[0, head_rows(h), lanes] = plain(k, change_full) * scale
            stacked[1, head_rows(h), lanes] = against_cols(q, change_full) * scale
            stacked[2, head_rows(h), lanes] = against_cols(d, unfolded(probs))
        return carry

    lax.fori_loop(0, heads, backward, 0, unroll=2)

    def tally(j, total):
        change = jnp.concatenate(
            [scores_grad[g, pl.ds(pl.multiple_of(j * heads, 8), heads), :] for g in range(blocks)],
            axis=1,
        )
        low = fold_low[pl.ds(j, 1), :]
        high = fold_high[pl.ds(j, 1), :]
        picked = jnp.concatenate(
            [jnp.where(high == c, change, 0.0) for c in range(table.shape[1])], axis=0
        ).astype(bf)
        mark = (lax.broadcasted_iota(jnp.int32, (128, rows), 0) == low).astype(f32).astype(bf)
        return total + against_cols(picked, mark)

    tallied = lax.fori_loop(
        0, fold, tally, jnp.zeros((table.shape[1] * heads, 128), f32), unroll=2
    )
    for c in range(table.shape[1]):
        small[pl.ds(0, heads), pl.ds(c * 128, 128)] = tallied[c * heads : (c + 1) * heads]

    normed1_grad = None
    for k in range(3):
        low = stacked[k].astype(bf)
        if k != 1:
            note(0 if k == 0 else 1, down_sum(jnp.transpose(low.astype(f32))))
        keep(grads.at[k], plain(low, act_rows), part)
        piece = transposed_left(low, weights[k])
        normed1_grad = piece if k == 0 else normed1_grad + piece
    note(4, down_sum(normed1_grad * normed[...]))
    note(5, down_sum(normed1_grad))
    embedded_grad = residual[...] + norm_through(normed1_grad, normed[...], inverse1, gain1)
    embedded_low = embedded_grad.astype(bf)
    input_grad[...] = embedded_low
    keep(table_grad, plain(onehot, embedded_low), table_grad.shape[-2])


def run_layer(
    planes, heads, features, graph_ids, degree, distance, out_grad, weights, table, bias, vectors, degree_table
):
    rows, width = features.shape
    block = graph_ids.shape[1]
    blocks = rows // block
    half = width // 2
    part = width // (planes * 4)
    table_part = degree_table.shape[0] // (planes * 4)
    small_rows = -(-(heads + 9) // 16) * 16
    bf, f32 = jnp.bfloat16, jnp.float32
    vmem = pl.BlockSpec(memory_space=pltpu.VMEM)
    return pl.pallas_call(
        functools.partial(layer_kernel, (planes, heads, width // heads, block, half)),
        out_shape=(
            jax.ShapeDtypeStruct((rows, width), bf),
            jax.ShapeDtypeStruct((rows, width), bf),
            jax.ShapeDtypeStruct((WEIGHTS, 2, 2, 2, planes, part, half), bf),
            jax.ShapeDtypeStruct((2, 2, 2, planes, table_part, half), bf),
            jax.ShapeDtypeStruct((small_rows, width), f32),
        ),
        in_specs=[vmem] * 10,
        out_specs=(vmem,) * 5,
        scratch_shapes=[
            pltpu.VMEM((rows, width), f32),
            pltpu.VMEM((rows, width), f32),
            pltpu.VMEM((rows, width), bf),
            pltpu.VMEM((3, width, rows), f32),
            pltpu.VMEM((width, rows), f32),
            pltpu.VMEM((blocks * heads, block // 2, block), f32),
            pltpu.VMEM((blocks, block // 2 * heads, block), f32),
            pltpu.VMEM((block // 2, rows), jnp.int32),
            pltpu.VMEM((block // 2, rows), jnp.int32),
            pltpu.VMEM((block // 2, rows), jnp.int32),
            pltpu.VMEM((rows, width), f32),
            pltpu.VMEM((rows, width), f32),
            pltpu.VMEM((rows, width), bf),
            pltpu.VMEM((width, rows), f32),
            pltpu.VMEM((3, width, rows), f32),
            pltpu.VMEM((rows, width), f32),
            pltpu.VMEM((width, 8), f32),
        ],
        name="layer",
    )(features, graph_ids, degree, distance, out_grad, weights, table, bias, vectors, degree_table)


def shards(
    planes,
    groups,
    node_features,
    graph_ids,
    degree,
    distance,
    out_grad,
    qkv_weight,
    qv_bias,
    out_weight,
    out_bias,
    norm1_gain,
    norm1_shift,
    ffn_in_weight,
    ffn_in_bias,
    ffn_out_weight,
    ffn_out_bias,
    norm2_gain,
    norm2_shift,
    degree_table,
    spatial_table,
):
    tensor = lax.axis_index("tensor")
    rows = node_features.shape[0]
    local_width = qkv_weight.shape[1]
    width = qkv_weight.shape[2]
    heads = spatial_table.shape[0] * planes
    table_rows = spatial_table.shape[1]

    bias_pack = jnp.pad(jnp.concatenate([qv_bias, ffn_in_bias[None]], axis=0), ((0, 5), (0, 0)))
    weights, whole_table, whole_bias = gather_weights(
        planes, qkv_weight, out_weight, ffn_in_weight, ffn_out_weight, spatial_table, bias_pack
    )
    vectors = jnp.stack(
        [out_bias, norm1_gain, norm1_shift, ffn_out_bias, norm2_gain, norm2_shift, out_bias, out_bias]
    )
    layer_out, input_grad, grads, degree_grad, small = run_layer(
        planes,
        heads,
        node_features,
        graph_ids,
        degree.reshape(1, rows),
        distance,
        out_grad,
        weights,
        whole_table.astype(jnp.float32).reshape(heads, table_rows // 128, 128),
        whole_bias,
        vectors,
        degree_table,
    )
    fin, fin_table, total = reduce_all(
        planes, groups, grads, degree_grad, small.astype(jnp.bfloat16)
    )

    def shard_of(piece):
        return piece.transpose(1, 2, 3, 0, 4).reshape(local_width, width).astype(jnp.float32)

    finished = [shard_of(fin[w]) for w in range(WEIGHTS)]
    table_grad = (
        fin_table.transpose(3, 1, 2, 4, 0, 5).reshape(degree_table.shape).astype(jnp.float32)
    )
    local_heads = spatial_table.shape[0]
    spatial_out = lax.dynamic_slice(
        total, (tensor * local_heads, 0), (local_heads, table_rows)
    )
    tail = total[heads : heads + 9]
    local = lax.dynamic_slice(tail, (0, tensor * local_width), (3, local_width))
    return (
        layer_out,
        input_grad,
        jnp.stack(finished[:3]),
        local[:2],
        finished[3],
        tail[3],
        tail[4],
        tail[5],
        finished[4],
        local[2],
        finished[5],
        tail[6],
        tail[7],
        tail[8],
        table_grad,
        spatial_out,
    )


def solution(mesh):
    planes = mesh.shape["tensor"]
    groups = mesh.shape["dp"] // 8
    return jax.shard_map(
        functools.partial(shards, planes, groups),
        mesh=mesh,
        in_specs=(
            P(("dp", "tensor"), None),
            P("dp", None),
            P(("dp", "tensor")),
            P("dp", None),
            P(("dp", "tensor"), None),
            P(None, "tensor", None),
            P(None, "tensor"),
            P("tensor", None),
            P(),
            P(),
            P(),
            P("tensor", None),
            P("tensor"),
            P("tensor", None),
            P(),
            P(),
            P(),
            P(),
            P("tensor", None),
        ),
        out_specs=(
            P(("dp", "tensor"), None),
            P(("dp", "tensor"), None),
            P(None, "tensor", None),
            P(None, "tensor"),
            P("tensor", None),
            P(),
            P(),
            P(),
            P("tensor", None),
            P("tensor"),
            P("tensor", None),
            P(),
            P(),
            P(),
            P(),
            P("tensor", None),
        ),
        check_vma=False,
    )
```

profile of v0, /device:TPU:0, one launch (start us, length us, event | category | flops | bytes accessed | tf_op | source)
XLA Modules:
  0.0 199.2 jit_solution(12473402675148293240)
XLA Ops:
  0.6 0.0 copy-start.2
  0.7 0.0 copy-start.3
  0.7 0.0 copy-start.4
  0.7 0.0 copy-start.5
  0.7 0.0 copy-start.6
  0.7 0.0 copy-start.7
  0.7 1.3 select_maximum_fusion.bias
  2.0 51.0 %gather_weights.1 = (bf16[6,4,2,2,48,768]{5,4,3,2,1,0:T(8,128)(2,1)}, bf16[4,8,512]{2,1,0:T(8,128)(2,1)}, f32[4,8,192]{2,1,0:T(8,128)}) custom-call(bf16[3,2,2,48,768]{4,3,2,1,0:T(8,128)(2,1)} %bitcast.56, bf16[2,2,48,768]{3,2,1,0:T(8,128)(2,1)} %bitcast.60, bf16[2,2,48,768]{3,2,1,0:T(8,128)(2,1)} %bitcast.61, bf16[2,2,48,768]{3,2,1,0:T(8,128)(2,1)} %bitcast.62, ...), custom_call_target="tpu_custom_call" | custom-call | tf_op jit(solution)/shard_map/gather_weights/pallas_call | solution.py:170
  53.1 1.4 reshape.128.table
  54.5 0.8 copy.36
  55.2 0.7 reshape.127.bias
  55.9 0.0 copy-done.2
  55.9 0.0 copy-done.3
  56.0 0.0 copy-done.4
  56.0 0.0 copy-done.5
  56.0 0.0 copy-done.6
  56.0 0.0 copy-done.7
  56.1 0.7 stack.38.vectors
  56.7 48.0 %layer.1 = (bf16[256,768]{1,0:T(8,128)(2,1)}, bf16[256,768]{1,0:T(8,128)(2,1)}, bf16[6,2,2,2,4,48,384]{6,5,4,3,2,1,0:T(8,128)(2,1)}, bf16[2,2,2,4,32,384]{5,4,3,2,1,0:T(8,128)(2,1)}, f32[48,768]{1,0:T(8,128)}) custom-call(bf16[256,768]{1,0:T(8,128)(2,1)} %features.1, s32[8,128]{1,0:T(8,128)} %graph_ids.1, s32[1,256]{1,0:T(1,128)} %bitcast.64, ...), custom_call_target="tpu_custom_call" | custom-call | tf_op jit(solution)/shard_map/layer/pallas_call | solution.py:703
  104.7 1.6 convert_element_type.110.small
  106.3 79.2 %reduce_grads.1 = (bf16[6,2,2,2,48,384]{5,4,3,2,1,0:T(8,128)(2,1)}, bf16[2,2,2,4,32,384]{5,4,3,2,1,0:T(8,128)(2,1)}, f32[48,768]{1,0:T(8,128)}) custom-call(bf16[6,2,2,2,4,48,384]{6,5,4,3,2,1,0:T(8,128)(2,1)} %get-tuple-element.32.grads, bf16[2,2,2,4,32,384]{5,4,3,2,1,0:T(8,128)(2,1)} %get-tuple-element.33.table, bf16[48,768]{1,0:T(8,128)(2,1)} %convert_element_type.110.small), custom_call_target="tpu_custom_call" | custom-call | tf_op jit(solution)/shard_map/reduce_grads/pallas_call | solution.py:419
  185.5 1.7 convert_bitcast_fusion.1
  187.2 0.3 copy.37
  187.5 0.2 convert_element_type.113
  187.7 0.3 copy.38
  188.0 0.2 convert_element_type.116
  188.2 0.3 copy.39
  188.5 0.0 copy-start.1
  188.5 0.2 convert_element_type.119
  188.7 1.3 maximum_convert_fusion
  190.1 0.0 copy-done.1
  190.1 0.7 constant_dynamic-slice_fusion
  190.7 0.6 dynamic-slice.1
  191.4 0.6 constant_dynamic-slice_fusion.1
  192.0 0.6 slice_reduce_fusion
  192.6 0.5 copy.40
  193.1 0.9 copy.44
  193.9 0.5 copy.41
  194.4 0.0 copy-start
  194.4 0.9 copy.45
  195.3 0.5 copy.42
  195.7 0.9 copy.46
  196.6 0.0 copy-done
  196.6 0.2 convert_bitcast_fusion
  196.8 1.2 copy.43
  198.0 1.2 copy.47
  (7 shorter events, 0.0 us)
Async XLA Ops:
  0.6 55.3 %copy-start.2 = (f32[768]{0:T(1024)S(1)}, f32[768]{0:T(1024)}, u32[]{:S(2)}) copy-start(f32[768]{0:T(1024)} %param.27) | copy-start | bytes 9220
  0.7 55.3 %copy-start.3 = (f32[768]{0:T(1024)S(1)}, f32[768]{0:T(1024)}, u32[]{:S(2)}) copy-start(f32[768]{0:T(1024)} %param.28) | copy-start | bytes 9220
  0.7 55.3 %copy-start.4 = (f32[768]{0:T(1024)S(1)}, f32[768]{0:T(1024)}, u32[]{:S(2)}) copy-start(f32[768]{0:T(1024)} %param.29) | copy-start | bytes 9220
  0.7 55.3 %copy-start.5 = (f32[768]{0:T(1024)S(1)}, f32[768]{0:T(1024)}, u32[]{:S(2)}) copy-start(f32[768]{0:T(1024)} %param.33) | copy-start | bytes 9220
  0.7 55.3 %copy-start.6 = (f32[768]{0:T(1024)S(1)}, f32[768]{0:T(1024)}, u32[]{:S(2)}) copy-start(f32[768]{0:T(1024)} %param.34) | copy-start | bytes 9220
  0.7 55.3 %copy-start.7 = (f32[768]{0:T(1024)S(1)}, f32[768]{0:T(1024)}, u32[]{:S(2)}) copy-start(f32[768]{0:T(1024)} %param.35) | copy-start | bytes 9220
  188.5 1.6 copy-start.1
  194.4 2.2 %copy-start = (bf16[2,2,2,4,32,384]{5,4,3,2,1,0:T(8,128)(2,1)S(1)}, bf16[2,2,2,4,32,384]{5,4,3,2,1,0:T(8,128)(2,1)}, u32[]{:S(2)}) copy-start(bf16[2,2,2,4,32,384]{5,4,3,2,1,0:T(8,128)(2,1)} %get-tuple-element.37) | copy-start | bytes 2359300
where the time goes:
time: 200 us; the launch traced here: 199 us
  Pallas kernels  178 us (89%)
  local copies, waits for them, and re-layouts  14 us (7%)
  other arithmetic  6.1 us (3%)
    pallas_call x1, Pallas kernels, reduce_all(): pl.pallas_call(functools.partial(reduce_kernel, planes, groups), out_shap...  79.2 us
    pallas_call x1, Pallas kernels, gather_weights(): pl.pallas_call(functools.partial(gather_kernel, planes, half), out_shape=...  51 us
    pallas_call x1, Pallas kernels, run_layer(): pl.pallas_call(functools.partial(layer_kernel, (planes, heads, width // h...  48 us

commit v1 on v0

--- a/solution.py
+++ b/solution.py
@@ -79,7 +79,6 @@
     )
     lanes = pl.ds(pl.multiple_of(core * half, half), half)
     shards = [qkv.at[0], qkv.at[1], qkv.at[2], out_w, in_w, ffn_w]
-    started = []
     small = []
     for k in range(1, planes):
         other = lax.rem(tensor + k, planes)
@@ -113,7 +112,7 @@
         locals_.append(pltpu.make_async_copy(shards[w], full.at[w, tensor], own_sem.at[w]))
     for copy in locals_:
         copy.start()
-    for w in range(WEIGHTS):
+    def to_second(w):
         first, second = (bit_x, bit_y) if w % 2 == 0 else (bit_y, bit_x)
         across = across_y if w % 2 == 0 else across_x
         for k in range(1, planes):
@@ -123,7 +122,8 @@
             stage_a[w, k] = send(
                 region, region, send_sem.at[1, w, k - 1], recv_sem.at[1, w, k - 1], (across, tensor)
             )
-    for w in range(WEIGHTS):
+
+    def to_first(w):
         first = bit_x if w % 2 == 0 else bit_y
         across = across_x if w % 2 == 0 else across_y
         for k in range(1, planes):
@@ -133,7 +133,8 @@
             stage_b[w, k] = send(
                 region, region, send_sem.at[2, w, k - 1], recv_sem.at[2, w, k - 1], (across, tensor)
             )
-    for w in range(WEIGHTS):
+
+    def to_core(w):
         for k in range(1, planes):
             stage_b[w, k].wait_recv()
             whose = lax.rem(tensor + planes - k, planes)
@@ -145,6 +146,12 @@
                 recv_sem.at[3, w, k - 1],
                 (across_core, tensor),
             )
+
+    for step in range(0, WEIGHTS + 4, 2):
+        for stage, late in ((to_core, 4), (to_first, 2), (to_second, 0)):
+            for w in (step - late, step - late + 1):
+                if 0 <= w < WEIGHTS:
+                    stage(w)
     for copy in small:
         copy.wait_recv()
     for copy in stage_c.values():
@@ -186,11 +193,7 @@
         compiler_params=pltpu.CompilerParams(collective_id=0, has_side_effects=True),
         name="gather_weights",
     )(split(qkv), split(out_w), split(in_w), split(ffn_w), table, bias)
-    return (
-        full.reshape(WEIGHTS, planes * shard_rows, width),
-        tables.reshape(-1, table.shape[1]),
-        biases.transpose(1, 0, 2).reshape(bias.shape[0], -1),
-    )
+    return full.reshape(WEIGHTS, planes * shard_rows, width), tables, biases
 
 
 def add_into(target, left, right):
@@ -256,15 +259,15 @@
 
     def small_job():
         copy = push(small, srecv_c, (across_core, tensor))
-        yield
+        yield True
         copy.wait_recv()
         add_into(ssum_a, small, srecv_c)
         copy = push(ssum_a, srecv_a, (across_x, tensor))
-        yield
+        yield True
         copy.wait_recv()
         add_into(ssum_b, ssum_a, srecv_a)
         copy = push(ssum_b, srecv_b, (across_y, tensor))
-        yield
+        yield True
         copy.wait_recv()
         add_into(ssum_z, ssum_b, srecv_b)
         srecv_z[tensor] = ssum_z[...]
@@ -272,7 +275,7 @@
             push(ssum_z, srecv_z.at[tensor], (dp, lax.rem(tensor + k, planes)))
             for k in range(1, planes)
         ]
-        yield
+        yield True
         for copy in sent:
             copy.wait_recv()
         total = srecv_z[0].astype(jnp.float32)
@@ -295,25 +298,25 @@
         first, second = (bit_x, bit_y) if x_first else (bit_y, bit_x)
         to_first, to_second = (across_x, across_y) if x_first else (across_y, across_x)
         copy = push(whole.at[1 - core], c_in, (across_core, tensor))
-        yield
+        yield True
         copy.wait_recv()
         own = whole.at[core]
         for p in range(planes):
             add_into(c_sum.at[:, :, p], own.at[:, :, p], c_in.at[:, :, p])
         copy = push(c_sum.at[1 - first], a_in, (to_first, tensor))
-        yield
+        yield True
         copy.wait_recv()
         for q in range(2):
             add_into(a_sum.at[q], c_sum.at[first, q], a_in.at[q])
         copy = push(a_sum.at[1 - second], b_in, (to_second, tensor))
-        yield
+        yield True
         copy.wait_recv()
         add_into(b_sum, a_sum.at[second], b_in)
         sent = []
         for k in range(1, planes):
             other = lax.rem(tensor + k, planes)
             sent.append(push(b_sum.at[other], z_in.at[k - 1], (dp, other)))
-        yield
+        yield True
         for copy in sent:
             copy.wait_recv()
         total = b_sum[tensor].astype(jnp.float32)
@@ -336,20 +339,20 @@
             sent = [
                 push(mine, mine, (dp, lax.rem(tensor + k, planes))) for k in range(1, planes)
             ]
-            yield
+            yield True
             for copy in sent:
                 copy.wait_recv()
         region = parts.at[core, first, second]
         copy = push(region, region, (to_second, tensor))
-        yield
+        yield True
         copy.wait_recv()
         region = parts.at[core, first]
         copy = push(region, region, (to_first, tensor))
-        yield
+        yield True
         copy.wait_recv()
         region = parts.at[core]
         copy = push(region, region, (across_core, tensor))
-        yield
+        yield True
         copy.wait_recv()
 
     jobs.append(small_job())
@@ -381,15 +384,11 @@
                 False,
             )
         )
-    while jobs:
-        left = []
-        for job in jobs:
-            try:
-                next(job)
-                left.append(job)
-            except StopIteration:
-                pass
-        jobs = left
+    waiting, running = jobs, []
+    while waiting or running:
+        enter = 4 if not running else 2
+        running, waiting = running + waiting[:enter], waiting[enter:]
+        running = [job for job in running if next(job, None)]
     for copy in copies:
         copy.wait_send()
 
@@ -473,15 +472,20 @@
     distance,
     out_grad,
     weights,
-    table,
-    bias,
-    vectors,
+    tables,
+    biases,
+    out_bias_in,
+    gain1_in,
+    shift1_in,
+    ffn_bias_in,
+    gain2_in,
+    shift2_in,
     degree_table,
     layer_out,
     input_grad,
     grads,
     table_grad,
-    small,
+    small_out,
     embedded,
     normed,
     act,
@@ -499,6 +503,8 @@
     stacked,
     pre_act,
     bias_cols,
+    table,
+    small,
 ):
     planes, heads, head_dim, block, half = shape
     rows, width = features.shape
@@ -508,7 +514,17 @@
     bf = jnp.bfloat16
     f32 = jnp.float32
     tensor = lax.axis_index("tensor")
-    out_bias, gain1, shift1, ffn_bias, gain2, shift2 = (vectors[pl.ds(n, 1), :] for n in range(6))
+    out_bias, gain1, shift1, ffn_bias, gain2, shift2 = (
+        given[...].reshape(1, width)
+        for given in (out_bias_in, gain1_in, shift1_in, ffn_bias_in, gain2_in, shift2_in)
+    )
+    local_heads = heads // planes
+    for p in range(planes):
+        local = tables[p].astype(f32)
+        for c in range(table.shape[1]):
+            table[pl.ds(p * local_heads, local_heads), c, :] = local[:, c * 128 : (c + 1) * 128]
+    bias = jnp.concatenate([biases[p] for p in range(planes)], axis=1)
+    lookups = table.shape[1]
 
     onehot = (
         lax.broadcasted_iota(jnp.int32, (degree_table.shape[0], rows), 0) == degree[...]
@@ -541,7 +557,7 @@
         down = folded(jnp.transpose(across))
         fold_same[:, lanes] = jnp.where(down == across[:fold], 1, 0)
 
-    bias_cols[...] = jnp.transpose(bias[...])
+    bias_cols[...] = jnp.transpose(bias)
     act_rows = act[...]
     for k in range(3):
         part = against_cols(weights[k], act_rows)
@@ -563,7 +579,7 @@
             low = fold_low[:, lanes]
             high = fold_high[:, lanes]
             looked = None
-            for c in range(table.shape[1]):
+            for c in range(lookups):
                 source = jnp.broadcast_to(table[h, pl.ds(c, 1), :], (fold, 128))
                 found = jnp.take_along_axis(source, low, axis=1, mode="promise_in_bounds")
                 looked = found if c == 0 else jnp.where(high == c, found, looked)
@@ -581,7 +597,7 @@
     again, inverse2 = normalized(residual[...])
     second[...] = again
     act2[...] = (again * gain2 + shift2).astype(bf)
-    pre_act[...] = against_cols(act2[...], weights[4]) + bias[pl.ds(2, 1), :]
+    pre_act[...] = against_cols(act2[...], weights[4]) + bias[2:3]
     upward = pre_act[...]
     bell = 0.5 * (1.0 + lax.erf(upward * (1.0 / math.sqrt(2.0))))
     hidden = (upward * bell).astype(bf)
@@ -605,7 +621,6 @@
     keep(grads.at[5], transposed_left(hidden, grad_low), part)
     keep(grads.at[4], transposed_left(pre_grad, act2[...]), part)
     small[...] = jnp.zeros_like(small)
-    table_width = table.shape[1] * 128
 
     def note(row, values):
         small[pl.ds(heads + row, 1), :] = values
@@ -661,15 +676,15 @@
         low = fold_low[pl.ds(j, 1), :]
         high = fold_high[pl.ds(j, 1), :]
         picked = jnp.concatenate(
-            [jnp.where(high == c, change, 0.0) for c in range(table.shape[1])], axis=0
+            [jnp.where(high == c, change, 0.0) for c in range(lookups)], axis=0
         ).astype(bf)
         mark = (lax.broadcasted_iota(jnp.int32, (128, rows), 0) == low).astype(f32).astype(bf)
         return total + against_cols(picked, mark)
 
     tallied = lax.fori_loop(
-        0, fold, tally, jnp.zeros((table.shape[1] * heads, 128), f32), unroll=2
-    )
-    for c in range(table.shape[1]):
+        0, fold, tally, jnp.zeros((lookups * heads, 128), f32), unroll=2
+    )
+    for c in range(lookups):
         small[pl.ds(0, heads), pl.ds(c * 128, 128)] = tallied[c * heads : (c + 1) * heads]
 
     normed1_grad = None
@@ -686,10 +701,11 @@
     embedded_low = embedded_grad.astype(bf)
     input_grad[...] = embedded_low
     keep(table_grad, plain(onehot, embedded_low), table_grad.shape[-2])
+    small_out[...] = small[...].astype(bf)
 
 
 def run_layer(
-    planes, heads, features, graph_ids, degree, distance, out_grad, weights, table, bias, vectors, degree_table
+    planes, heads, features, graph_ids, degree, distance, out_grad, weights, tables, biases, vectors, degree_table
 ):
     rows, width = features.shape
     block = graph_ids.shape[1]
@@ -707,9 +723,9 @@
             jax.ShapeDtypeStruct((rows, width), bf),
             jax.ShapeDtypeStruct((WEIGHTS, 2, 2, 2, planes, part, half), bf),
             jax.ShapeDtypeStruct((2, 2, 2, planes, table_part, half), bf),
-            jax.ShapeDtypeStruct((small_rows, width), f32),
+            jax.ShapeDtypeStruct((small_rows, width), bf),
         ),
-        in_specs=[vmem] * 10,
+        in_specs=[vmem] * 15,
         out_specs=(vmem,) * 5,
         scratch_shapes=[
             pltpu.VMEM((rows, width), f32),
@@ -729,9 +745,80 @@
             pltpu.VMEM((3, width, rows), f32),
             pltpu.VMEM((rows, width), f32),
             pltpu.VMEM((width, 8), f32),
+            pltpu.VMEM((heads, tables.shape[2] // 128, 128), f32),
+            pltpu.VMEM((small_rows, width), f32),
         ],
         name="layer",
-    )(features, graph_ids, degree, distance, out_grad, weights, table, bias, vectors, degree_table)
+    )(features, graph_ids, degree, distance, out_grad, weights, tables, biases, *vectors, degree_table)
+
+
+def finish_kernel(
+    shape,
+    fin,
+    fin_table,
+    total,
+    qkv_out,
+    qv_out,
+    out_w_out,
+    ffn_in_out,
+    ffn_in_b_out,
+    ffn_out_out,
+    table_out,
+    spatial_out,
+    *vector_outs,
+):
+    planes, heads, local_width = shape
+    part, half = fin.shape[-2:]
+    table_part = fin_table.shape[-2]
+    f32 = jnp.float32
+    tensor = lax.axis_index("tensor")
+    targets = [qkv_out.at[0], qkv_out.at[1], qkv_out.at[2], out_w_out, ffn_in_out, ffn_out_out]
+    for c in range(2):
+        lanes = pl.ds(c * half, half)
+        for a in range(2):
+            for b in range(2):
+                at = pl.ds((a * 2 + b) * part, part)
+                for w, target in enumerate(targets):
+                    target[at, lanes] = fin[w, c, a, b].astype(f32)
+                for p in range(planes):
+                    at_table = pl.ds(((p * 2 + a) * 2 + b) * table_part, table_part)
+                    table_out[at_table, lanes] = fin_table[c, a, b, p].astype(f32)
+    local_heads = heads // planes
+    spatial_out[...] = total[
+        pl.ds(pl.multiple_of(tensor * local_heads, 8), local_heads), pl.ds(0, spatial_out.shape[1])
+    ]
+    rows = total[pl.ds(heads, 16), :]
+    own = rows[:, :local_width]
+    for p in range(1, planes):
+        own = jnp.where(tensor == p, rows[:, p * local_width : (p + 1) * local_width], own)
+    qv_out[...] = own[:2]
+    ffn_in_b_out[...] = own[2]
+    for n, target in enumerate(vector_outs):
+        target[...] = rows[3 + n]
+
+
+def finish(planes, heads, local_width, degrees, table_rows, fin, fin_table, total):
+    width = total.shape[1]
+    f32 = jnp.float32
+    vmem = pl.BlockSpec(memory_space=pltpu.VMEM)
+    matrix = jax.ShapeDtypeStruct((local_width, width), f32)
+    return pl.pallas_call(
+        functools.partial(finish_kernel, (planes, heads, local_width)),
+        out_shape=(
+            jax.ShapeDtypeStruct((3, local_width, width), f32),
+            jax.ShapeDtypeStruct((2, local_width), f32),
+            matrix,
+            matrix,
+            jax.ShapeDtypeStruct((local_width,), f32),
+            matrix,
+            jax.ShapeDtypeStruct((degrees, width), f32),
+            jax.ShapeDtypeStruct((heads // planes, table_rows), f32),
+        )
+        + (jax.ShapeDtypeStruct((width,), f32),) * 6,
+        in_specs=[vmem] * 3,
+        out_specs=(vmem,) * 14,
+        name="finish",
+    )(fin, fin_table, total)
 
 
 def shards(
@@ -765,11 +852,8 @@
     table_rows = spatial_table.shape[1]
 
     bias_pack = jnp.pad(jnp.concatenate([qv_bias, ffn_in_bias[None]], axis=0), ((0, 5), (0, 0)))
-    weights, whole_table, whole_bias = gather_weights(
+    weights, tables, biases = gather_weights(
         planes, qkv_weight, out_weight, ffn_in_weight, ffn_out_weight, spatial_table, bias_pack
-    )
-    vectors = jnp.stack(
-        [out_bias, norm1_gain, norm1_shift, ffn_out_bias, norm2_gain, norm2_shift, out_bias, out_bias]
     )
     layer_out, input_grad, grads, degree_grad, small = run_layer(
         planes,
@@ -780,44 +864,34 @@
         distance,
         out_grad,
         weights,
-        whole_table.astype(jnp.float32).reshape(heads, table_rows // 128, 128),
-        whole_bias,
-        vectors,
+        tables,
+        biases,
+        (out_bias, norm1_gain, norm1_shift, ffn_out_bias, norm2_gain, norm2_shift),
         degree_table,
     )
     fin, fin_table, total = reduce_all(
-        planes, groups, grads, degree_grad, small.astype(jnp.bfloat16)
-    )
-
-    def shard_of(piece):
-        return piece.transpose(1, 2, 3, 0, 4).reshape(local_width, width).astype(jnp.float32)
-
-    finished = [shard_of(fin[w]) for w in range(WEIGHTS)]
-    table_grad = (
-        fin_table.transpose(3, 1, 2, 4, 0, 5).reshape(degree_table.shape).astype(jnp.float32)
-    )
-    local_heads = spatial_table.shape[0]
-    spatial_out = lax.dynamic_slice(
-        total, (tensor * local_heads, 0), (local_heads, table_rows)
-    )
-    tail = total[heads : heads + 9]
-    local = lax.dynamic_slice(tail, (0, tensor * local_width), (3, local_width))
+        planes, groups, grads, degree_grad, small
+    )
+
+    finished = finish(planes, heads, local_width, degree_table.shape[0], table_rows, fin, fin_table, total)
+    qkv_out, qv_out, out_w_out, ffn_in_out, ffn_in_b_out, ffn_out_out, table_out, spatial_out = finished[:8]
+    out_b_out, gain1_out, shift1_out, ffn_b_out, gain2_out, shift2_out = finished[8:]
     return (
         layer_out,
         input_grad,
-        jnp.stack(finished[:3]),
-        local[:2],
-        finished[3],
-        tail[3],
-        tail[4],
-        tail[5],
-        finished[4],
-        local[2],
-        finished[5],
-        tail[6],
-        tail[7],
-        tail[8],
-        table_grad,
+        qkv_out,
+        qv_out,
+        out_w_out,
+        out_b_out,
+        gain1_out,
+        shift1_out,
+        ffn_in_out,
+        ffn_in_b_out,
+        ffn_out_out,
+        ffn_b_out,
+        gain2_out,
+        shift2_out,
+        table_out,
         spatial_out,
     )
 

time: 200 us -> 168 us (0.84)
  local copies, waits for them, and re-layouts: 14 us -> 0 us
  Pallas kernels: 178 us -> 166 us
  other arithmetic: 6.1 us -> 1.3 us
    pallas_call x1, Pallas kernels: 79.2 us -> 67.4 us  [reduce_all(): pl.pallas_call(functools.partial(reduce_kernel, planes, groups), out_shap...]
    pallas_call x1, Pallas kernels: 51 us -> 45.5 us  [gather_weights(): pl.pallas_call(functools.partial(gather_kernel, planes, half), out_shape=...]
    convert_element_type x11 -> x0, local copies, waits for them, and re-layouts: 5.48 us -> none  [the longest x9 2.85 us: shard_of(): piece.transpose(1, 2, 3, 0, 4).reshape(local_width, width)]
    pallas_call x0 -> x1, Pallas kernels: none -> 4.34 us  [finish(): pl.pallas_call(functools.partial(finish_kernel, (planes, heads, local_wid...]
    unnamed x20 -> x0, local copies, waits for them, and re-layouts: 3.84 us -> none
    convert_element_type x3 -> x0, other arithmetic: 3.41 us -> none  [the longest x1 1.67 us: shard_of(): piece.transpose(1, 2, 3, 0, 4).reshape(local_width, width)]
where the time goes in v1:
time: 168 us
  Pallas kernels  166 us (99%)
    pallas_call x1, Pallas kernels, reduce_all(): pl.pallas_call(functools.partial(reduce_kernel, planes, groups), out_shap...  67.4 us
    pallas_call x1, Pallas kernels, run_layer(): pl.pallas_call(functools.partial(layer_kernel, (planes, heads, width // h...  48.3 us
    pallas_call x1, Pallas kernels, gather_weights(): pl.pallas_call(functools.partial(gather_kernel, planes, half), out_shape=...  45.5 us
    pallas_call x1, Pallas kernels, finish(): pl.pallas_call(functools.partial(finish_kernel, (planes, heads, local_wid...  4.34 us

profile of v1, /device:TPU:0, one launch (start us, length us, event | category | flops | bytes accessed | tf_op | source)
XLA Modules:
  0.0 167.7 jit_solution(14338172191382101615)
XLA Ops:
  0.6 1.3 select_maximum_fusion.bias
  2.0 45.5 %gather_weights.1 = (bf16[6,4,2,2,48,768]{5,4,3,2,1,0:T(8,128)(2,1)}, bf16[4,8,512]{2,1,0:T(8,128)(2,1)}, f32[4,8,192]{2,1,0:T(8,128)}) custom-call(bf16[3,2,2,48,768]{4,3,2,1,0:T(8,128)(2,1)} %bitcast.8, bf16[2,2,48,768]{3,2,1,0:T(8,128)(2,1)} %bitcast.9, bf16[2,2,48,768]{3,2,1,0:T(8,128)(2,1)} %bitcast.10, bf16[2,2,48,768]{3,2,1,0:T(8,128)(2,1)} %bitcast.11, ...), custom_call_target="tpu_custom_call" | custom-call | tf_op jit(solution)/shard_map/gather_weights/pallas_call | solution.py:177
  47.5 48.3 %layer.1 = (bf16[256,768]{1,0:T(8,128)(2,1)}, bf16[256,768]{1,0:T(8,128)(2,1)}, bf16[6,2,2,2,4,48,384]{6,5,4,3,2,1,0:T(8,128)(2,1)}, bf16[2,2,2,4,32,384]{5,4,3,2,1,0:T(8,128)(2,1)}, bf16[48,768]{1,0:T(8,128)(2,1)}) custom-call(bf16[256,768]{1,0:T(8,128)(2,1)} %features.1, s32[8,128]{1,0:T(8,128)} %graph_ids.1, s32[1,256]{1,0:T(1,128)} %bitcast.13, ...), custom_call_target="tpu_custom_call" | custom-call | tf_op jit(solution)/shard_map/layer/pallas_call | solution.py:719
  95.8 67.4 %reduce_grads.1 = (bf16[6,2,2,2,48,384]{5,4,3,2,1,0:T(8,128)(2,1)}, bf16[2,2,2,4,32,384]{5,4,3,2,1,0:T(8,128)(2,1)}, f32[48,768]{1,0:T(8,128)}) custom-call(bf16[6,2,2,2,4,48,384]{6,5,4,3,2,1,0:T(8,128)(2,1)} %get-tuple-element.46.grads, bf16[2,2,2,4,32,384]{5,4,3,2,1,0:T(8,128)(2,1)} %get-tuple-element.47.table, bf16[48,768]{1,0:T(8,128)(2,1)} %get-tuple-element.48.small), custom_call_target="tpu_custom_call" | custom-call | tf_op jit(solution)/shard_map/reduce_grads/pallas_call | solution.py:418
  163.2 4.3 %finish.1 = (f32[3,192,768]{2,1,0:T(8,128)}, f32[2,192]{1,0:T(2,128)}, f32[192,768]{1,0:T(8,128)}, f32[192,768]{1,0:T(8,128)}, f32[192]{0:T(256)}, /*index=5*/f3...) custom-call(bf16[6,2,2,2,48,384]{5,4,3,2,1,0:T(8,128)(2,1)} %get-tup, ...), custom_call_target="tpu_custom_call" | custom-call | tf_op jit(solution)/shard_map/finish/pallas_call | solution.py:805
